TPU v7x, 32 devices: a whole 2x2x4 slice. The times are simulated.
32 devices in a mesh: dp: 4 (over x, core), expert: 8 (over z, y).
Axes of the slice: x: 2, y: 2, z: 4, core: 2. Of those that a mesh axis runs over, the one named last changes fastest.
Arguments:
- tokens: bfloat16 [128, 256, 1280], P(('dp', 'expert')), may hold values from -32 to 32
- slot_keys: bfloat16 [1280, 8], replicated, may hold values from -20 to 20
- logit_scale: float32 [1], replicated, may hold values from 8 to 16
- up_weight: bfloat16 [8, 1280, 5120], P('expert', None, 'dp'), may hold values from -0.15625 to 0.15625
- up_bias: bfloat16 [8, 5120], P('expert', 'dp'), may hold values from -3 to 3
- down_weight: bfloat16 [8, 5120, 1280], P('expert', 'dp'), may hold values from -0.078125 to 0.078125
- down_bias: bfloat16 [8, 1280], replicated, may hold values from -3 to 3
Outputs:
- mixed_out: bfloat16 [128, 256, 1280], P(('dp', 'expert'))
All inputs are finite; a program needn't handle non-finite values.
Results may differ from a plain program's by a relative error of at most 0.017.
Values may be sent and summed in bfloat16 or wider, within the bound.
A program may use at most 64 MiB of HBM per device.

v0:
```python
import jax
import jax.numpy as jnp
from jax import lax
from jax.sharding import PartitionSpec as P

norm_eps = 1e-06


def unit_rms(values, axis_pos):
    return values * lax.rsqrt(jnp.mean(values * values, axis=axis_pos, keepdims=True) + norm_eps)


def body(tokens, slot_keys, logit_scale, up_weight, up_bias, down_weight, down_bias):
    images = tokens.shape[0]
    patches = tokens.shape[1]
    width = tokens.shape[2]
    per_owner = up_weight.shape[0]
    owners = lax.axis_size("expert")
    normed_tok = unit_rms(tokens.astype(jnp.float32), 2).astype(jnp.bfloat16)
    normed_keys = unit_rms(slot_keys.astype(jnp.float32), 0).astype(jnp.bfloat16)
    raw_scores = jnp.einsum(
        "ipd,dn->inp", normed_tok, normed_keys, preferred_element_type=jnp.float32
    )
    logits = logit_scale[0] * raw_scores / width
    dispatch = jax.nn.softmax(logits, axis=2).astype(jnp.bfloat16)
    combine = jax.nn.softmax(logits, axis=1).astype(jnp.bfloat16)
    slot_inputs = jnp.einsum(
        "inp,ipd->ind", dispatch, tokens, preferred_element_type=jnp.float32
    ).astype(jnp.bfloat16)
    routed = lax.all_to_all(slot_inputs, "expert", split_axis=1, concat_axis=0, tiled=True)
    pre = jnp.einsum(
        "rkd,kdf->rkf",
        lax.all_gather(routed, "dp", axis=0, tiled=True),
        up_weight,
        preferred_element_type=jnp.float32,
    )
    pre = pre + up_bias.astype(jnp.float32)[None]
    hidden = jax.nn.gelu(pre, approximate=False).astype(jnp.bfloat16)
    summed = lax.psum_scatter(
        jnp.einsum("rkf,kfd->rkd", hidden, down_weight, preferred_element_type=jnp.float32).astype(
            jnp.bfloat16
        ),
        "dp",
        scatter_dimension=0,
        tiled=True,
    ).astype(jnp.float32)
    own_bias = lax.dynamic_slice_in_dim(
        down_bias, lax.axis_index("expert") * per_owner, per_owner, 0
    ).astype(jnp.float32)
    finished = (
        (summed + own_bias[None]).astype(jnp.bfloat16).reshape(owners, images, per_owner, width)
    )
    returned = lax.all_to_all(finished, "expert", split_axis=0, concat_axis=0, tiled=True)
    weights = combine.reshape(images, owners, per_owner, patches)
    mixed_out = jnp.einsum("iekp,eikd->ipd", weights, returned, preferred_element_type=jnp.float32)
    return mixed_out.astype(jnp.bfloat16)


def solution(mesh):
    return jax.shard_map(
        body,
        mesh=mesh,
        in_specs=(
            P(("dp", "expert"), None, None),
            P(),
            P(),
            P("expert", None, "dp"),
            P("expert", "dp"),
            P("expert", "dp", None),
            P(),
        ),
        out_specs=P(("dp", "expert"), None, None),
        check_vma=False,
    )
```

profile of v0, /device:TPU:0, one launch (start us, length us, event | category | flops | bytes accessed | tf_op | source)
XLA Modules:
  0.0 83.9 jit_solution(10107239753829949492)
XLA Ops:
  6.5 0.0 copy-start
  7.3 1.0 %fusion.96 = f32[8]{0:T(128)S(1)} fusion(bf16[1280,8]{0,1:T(8,128)(2,1)} %param.8), kind=kLoop, calls=%fused_computation.87 | loop fusion | flops 30712 | bytes 20512 | tf_op jit(solution)/shard_map/reduce_sum | solution.py:10
  8.4 2.3 %fusion.2 = f32[4,256]{1,0:T(4,128)S(1)} fusion(bf16[4,256,1280]{2,1,0:T(8,128)(2,1)} %param.7), kind=kLoop, calls=%fused_computation.4 | loop fusion | flops 3931136 | bytes 2625536 | tf_op jit(solution)/shard_map/reduce_sum | solution.py:10
  10.7 0.0 copy-start.1
  10.7 2.6 %fusion.33 = f32[4,8,256]{2,1,0:T(8,128)S(1)} fusion(bf16[4,256,1280]{2,1,0:T(8,128)(2,1)} %param.7, f32[4,256]{1,0:T(4,128)S(1)} %add_rsqrt_fusion, bf16[1280,8]{0,1:T(8,128)(2,1)} %param.8, f32[8]{0:T(128)S(1)} %add_rsqrt_fusion.1, f32[]{:T(128)} %bitcast.139), kind=kOutput, calls=%fused_computation.24 | convolution fusion | flops 24950784 | bytes 2678820 | tf_op jit(solution)/shard_map/ipd,dn->inp/dot_general | solution.py:21
  13.3 0.2 fusion.133
  13.5 2.2 %convolution_convert_fusion.1 = bf16[4,8,1280]{2,1,0:T(8,128)(2,1)S(1)} fusion(bf16[4,256,1280]{2,1,0:T(8,128)(2,1)} %param.7, f32[4,8]{1,0:T(4,128)S(1)} %fusion.133, f32[4,8,256]{2,1,0:T(8,128)S(1)} %fusion.33), kind=kOutput, calls=%fused_computation.17 | convolution fusion | flops 21037344 | bytes 2736256 | tf_op jit(solution)/shard_map/inp,ipd->ind/dot_general | solution.py:27
  15.8 0.7 copy.11
  16.4 7.3 %all-to-all-start = ((bf16[4,8,1280]{2,0,1:T(4,128)(2,1)}), bf16[4,8,1280]{2,0,1:T(4,128)(2,1)S(1)}, u32[]{:S(2)}, u32[]{:S(2)}) async-start(bf16[4,8,1280]{2,0,1:T(4,128)(2,1)} %copy.11), calls=%async_computation | async-start | bytes 163840 | tf_op jit(solution)/shard_map/all_to_all | solution.py:30
  23.7 0.0 reduce-scatter.2.cloned.1.call-start
  23.8 0.0 copy-done.1
  23.8 6.9 %all-to-all-done = bf16[4,8,1280]{2,0,1:T(4,128)(2,1)S(1)} async-done(((bf16[4,8,1280]{2,0,1:T(4,128)(2,1)}), bf16[4,8,1280]{2,0,1:T(4,128)(2,1)S(1)}, u32[]{:S(2)}, u32[]{:S(2)}) %all-to-all-start) | async-done | bytes 81952 | tf_op jit(solution)/shard_map/all_to_all | solution.py:30
  30.8 6.6 %all_gather.3 = bf16[128,1,1280]{2,0,1:T(8,128)(2,1)} all-gather(bf16[32,1,1280]{2,0,1:T(8,128)(2,1)S(1)} %all_to_all.19), channel_id=1, replica_groups=mesh['dp'=4,'expert'=8] {'dp'}, dimensions={0}, use_global_device_ids=true | all-gather | bytes 409600 | tf_op jit(solution)/shard_map/all_gather | solution.py:33
  37.3 0.0 copy-done
  37.3 5.2 %fusion.20 = bf16[128,1,1280]{2,0,1:T(8,128)(2,1)} fusion(bf16[1,1280,1280]{2,1,0:T(8,128)(2,1)S(1)} %copy-done, bf16[1,1280,1280]{2,1,0:T(8,128)(2,1)} %param.10, bf16[128,1,1280]{2,0,1:T(8,128)(2,1)} %all_gather.3, f32[1280]{0:T(1024)S(1)} %convert_reduce_fusion.1), kind=kOutput, calls=%fused_computation.16 | convolution fusion | flops 849838080 | bytes 7214080 | tf_op jit(solution)/shard_map/rkf,kfd->rkd/dot_general | solution.py:40
  42.6 0.0 reduce-scatter.2.cloned.1.call-update
  42.6 0.8 convert_reduce_fusion
  43.3 17.3 %reduce-scatter.2.cloned.1.call-done = bf16[32,1,1280]{2,0,1:T(8,128)(2,1)} async-done(((bf16[128,1,1280]{2,0,1:T(8,128)(2,1)}), bf16[32,1,1280]{2,0,1:T(8,128)(2,1)}) %reduce-scatter.2.cloned.1.call-update) | async-done | bytes 81936 | tf_op jit(solution)/shard_map/reduce_scatter | solution.py:39
  60.6 0.9 %add_convert_fusion = bf16[32,1,1280]{2,0,1:T(8,128)(2,1)S(1)} fusion(bf16[32,1,1280]{2,0,1:T(8,128)(2,1)} %reduce-scatter.2.cloned.1.call-done, f32[1280]{0:T(1024)S(1)} %convert_reduce_fusion), kind=kLoop, calls=%fused_computation.82 | loop fusion | flops 122880 | bytes 168960 | tf_op jit(solution)/shard_map/convert_element_type | solution.py:51
  61.5 0.7 reshape.56
  62.2 5.5 %all-to-all-start.1 = ((bf16[8,4,1,1280]{3,1,2,0:T(4,128)(2,1)}), bf16[8,4,1,1280]{3,1,2,0:T(4,128)(2,1)S(1)}, u32[]{:S(2)}, u32[]{:S(2)}) async-start(bf16[8,4,1,1280]{3,1,2,0:T(4,128)(2,1)} %bitcast.16), calls=%async_computation.2 | async-start | bytes 163840 | tf_op jit(solution)/shard_map/all_to_all | solution.py:53
  67.7 7.0 %all-to-all-done.1 = bf16[8,4,1,1280]{3,1,2,0:T(4,128)(2,1)S(1)} async-done(((bf16[8,4,1,1280]{3,1,2,0:T(4,128)(2,1)}), bf16[8,4,1,1280]{3,1,2,0:T(4,128)(2,1)S(1)}, u32[]{:S(2)}, u32[]{:S(2)}) %all-to-all-start.1) | async-done | bytes 81952 | tf_op jit(solution)/shard_map/all_to_all | solution.py:53
  74.7 2.4 %convolution_convert_fusion = bf16[4,256,1280]{2,1,0:T(8,128)(2,1)} fusion(bf16[8,4,1,1280]{3,1,2,0:T(4,128)(2,1)S(1)} %all-to-all-done.1, f32[4,256]{1,0:T(4,128)S(1)} %fusion.134, f32[4,8,256]{2,1,0:T(8,128)S(1)} %fusion.33), kind=kOutput, calls=%fused_computation.6 | convolution fusion | flops 22307848 | bytes 2740224 | tf_op jit(solution)/shard_map/iekp,eikd->ipd/dot_general | solution.py:55
  (5 shorter events, 0.1 us)
Async XLA Ops:
  6.5 30.8 %copy-start = (bf16[1,1280,1280]{2,1,0:T(8,128)(2,1)S(1)}, bf16[1,1280,1280]{2,1,0:T(8,128)(2,1)}, u32[]{:S(2)}) copy-start(bf16[1,1280,1280]{2,1,0:T(8,128)(2,1)} %param.12) | copy-start | bytes 9830404
  10.7 13.1 %copy-start.1 = (bf16[1,1280]{1,0:T(2,128)(2,1)S(1)}, bf16[1,1280]{1,0:T(2,128)(2,1)}, u32[]{:S(2)}) copy-start(bf16[1,1280]{1,0:T(2,128)(2,1)} %param.11) | copy-start | bytes 7684
  16.4 14.3 %all-to-all-start = ((bf16[4,8,1280]{2,0,1:T(4,128)(2,1)}), bf16[4,8,1280]{2,0,1:T(4,128)(2,1)S(1)}, u32[]{:S(2)}, u32[]{:S(2)}) async-start(bf16[4,8,1280]{2,0,1:T(4,128)(2,1)} %copy.11), calls=%async_computation | async-start | bytes 163840 | tf_op jit(solution)/shard_map/all_to_all | solution.py:30
  23.7 36.9 %reduce-scatter.2.cloned.1.call-start = ((), (), s32[]{:S(2)}) async-start(), calls=%async_computation.3 | async-start | bytes 409600 | tf_op jit(solution)/shard_map/reduce_scatter | solution.py:39
  62.2 12.5 %all-to-all-start.1 = ((bf16[8,4,1,1280]{3,1,2,0:T(4,128)(2,1)}), bf16[8,4,1,1280]{3,1,2,0:T(4,128)(2,1)S(1)}, u32[]{:S(2)}, u32[]{:S(2)}) async-start(bf16[8,4,1,1280]{3,1,2,0:T(4,128)(2,1)} %bitcast.16), calls=%async_computation.2 | async-start | bytes 163840 | tf_op jit(solution)/shard_map/all_to_all | solution.py:53
Sparse Core Ops, SparseCore 0:
  42.7 17.8 reduce-scatter.1
where the time goes:
time: 84.4 us; the launch traced here: 83.9 us
  waiting for transfers between devices  31.2 us (37%)
  between operations  14.2 us (17%)
  starting transfers between devices  12.8 us (15%)
  matrix products  12.5 us (15%)
  blocking collectives  6.55 us (8%)
  other arithmetic  5.26 us (6%)
  local copies, waits for them, and re-layouts  1.37 us (2%)
    reduce_scatter x1, waiting for transfers between devices, body(): lax.psum_scatter(jnp.einsum('rkf,kfd->rkd', hidden, down_weight, preferre...  17.3 us
    all_to_all x1, starting transfers between devices, body(): lax.all_to_all(slot_inputs, 'expert', split_axis=1, concat_axis=0, tiled=...  7.31 us
    all_to_all x1, waiting for transfers between devices, body(): lax.all_to_all(finished, 'expert', split_axis=0, concat_axis=0, tiled=True)  6.98 us
    all_to_all x1, waiting for transfers between devices, body(): lax.all_to_all(slot_inputs, 'expert', split_axis=1, concat_axis=0, tiled=...  6.93 us
    all_gather x1, blocking collectives, body(): lax.all_gather(routed, 'dp', axis=0, tiled=True)  6.55 us
    all_to_all x1, starting transfers between devices, body(): lax.all_to_all(finished, 'expert', split_axis=0, concat_axis=0, tiled=True)  5.5 us
    dot_general x1, matrix products, body(): jnp.einsum('rkf,kfd->rkd', hidden, down_weight, preferred_element_type=jn...  5.22 us
    reduce_sum x2, other arithmetic, unit_rms(): jnp.mean(values * values, axis=axis_pos, keepdims=True) + norm_eps  3.35 us
  transfers between devices with their start and end apart: 3, of which 3 were waited for; matrix products, arithmetic and copies ran while one was open for 1% of the time, Pallas kernels for 0%

commit v1 on v0

--- a/solution.py
+++ b/solution.py
@@ -4,6 +4,13 @@
 from jax.sharding import PartitionSpec as P
 
 norm_eps = 1e-06
+
+
+def measure_the_panel(local_array, dim_at):
+    local_array = jnp.moveaxis(local_array, 0, dim_at)
+    z1 = local_array.shape
+    oldest = local_array.reshape(*z1[:dim_at], z1[dim_at] * z1[dim_at + 1], *z1[dim_at + 2 :])
+    return oldest
 
 
 def unit_rms(values, axis_pos):
@@ -28,12 +35,32 @@
         "inp,ipd->ind", dispatch, tokens, preferred_element_type=jnp.float32
     ).astype(jnp.bfloat16)
     routed = lax.all_to_all(slot_inputs, "expert", split_axis=1, concat_axis=0, tiled=True)
-    pre = jnp.einsum(
-        "rkd,kdf->rkf",
-        lax.all_gather(routed, "dp", axis=0, tiled=True),
-        up_weight,
-        preferred_element_type=jnp.float32,
-    )
+    local_now = lax.axis_size("dp")
+    reply = lax.axis_index("dp")
+    field_out, v_next, vec_out = (local_now, reply, routed.shape[0])
+    pages = [(no, (no + 1) % field_out) for no in range(field_out)]
+    chunks = [(no, (no - 1) % field_out) for no in range(field_out)]
+    small = field_out // 2
+    current_value = {}
+    finding = outcome_arr = routed
+    for k0 in range(small + 1):
+        state_next = lax.ppermute(finding, axis_name="dp", perm=pages) if k0 < small else None
+        before = (
+            lax.ppermute(outcome_arr, axis_name="dp", perm=chunks)
+            if k0 < field_out - small - 1
+            else None
+        )
+        current_value[-k0] = jnp.einsum(
+            "rkd,kdf->rkf", finding, up_weight, preferred_element_type=jnp.float32
+        )
+        if 0 < k0 < field_out - small:
+            current_value[k0] = jnp.einsum(
+                "rkd,kdf->rkf", outcome_arr, up_weight, preferred_element_type=jnp.float32
+            )
+        finding, outcome_arr = (state_next, before)
+    current_value = jnp.stack([current_value[i0] for i0 in sorted(current_value)])
+    current_value = current_value[(jnp.arange(field_out) - v_next + small) % field_out]
+    pre = measure_the_panel(current_value, 0)
     pre = pre + up_bias.astype(jnp.float32)[None]
     hidden = jax.nn.gelu(pre, approximate=False).astype(jnp.bfloat16)
     summed = lax.psum_scatter(

time: 84.4 us -> 90.8 us (1.076)
  blocking collectives: 6.55 us -> 0 us
  other arithmetic: 5.26 us -> 9.84 us
  waiting for transfers between devices: 31.2 us -> 35.4 us
  local copies, waits for them, and re-layouts: 1.37 us -> 4.03 us
    all_gather x1 -> x0, blocking collectives: 6.55 us -> none  [body(): lax.all_gather(routed, 'dp', axis=0, tiled=True)]
    ppermute x0 -> x3, waiting for transfers between devices: none -> 6.08 us  [the longest x2 6.08 us: body(): lax.ppermute(finding, axis_name='dp', perm=pages)]
    convert_element_type x0 -> x2, other arithmetic: none -> 3.1 us  [the longest x1 2.51 us: body(): hidden = jax.nn.gelu(pre, approximate=False).astype(jnp.bfloat16)]
    dot_general x0 -> x4, matrix products: none -> 2.73 us  [the longest x3 2.04 us: body(): jnp.einsum('rkd,kdf->rkf', finding, up_weight, preferred_element_type=jnp...]
    gather x0 -> x1, local copies, waits for them, and re-layouts: none -> 2.63 us  [body(): current_value[(jnp.arange(field_out) - v_next + small) % field_out]]
    dot_general x1, matrix products: 5.22 us -> 3.26 us  [body(): jnp.einsum('rkf,kfd->rkd', hidden, down_weight, preferred_element_type=jn...]
    all_to_all x1, waiting for transfers between devices: 6.93 us -> 5.75 us  [body(): lax.all_to_all(slot_inputs, 'expert', split_axis=1, concat_axis=0, tiled=...]
  transfers between devices with their start and end apart: 3 -> 6, of which waited for: 3 -> 5; matrix products, arithmetic and copies ran while one was open for 1% -> 4% of each run, Pallas kernels for 0% -> 0%
where the time goes in v1:
time: 90.8 us; the launch traced here: 90.2 us
  waiting for transfers between devices  35.4 us (39%)
  between operations  14.3 us (16%)
  starting transfers between devices  13.4 us (15%)
  matrix products  13.2 us (15%)
  other arithmetic  9.84 us (11%)
  local copies, waits for them, and re-layouts  4.03 us (4%)
    reduce_scatter x1, waiting for transfers between devices, body(): lax.psum_scatter(jnp.einsum('rkf,kfd->rkd', hidden, down_weight, preferre...  16.5 us
    all_to_all x1, starting transfers between devices, body(): lax.all_to_all(slot_inputs, 'expert', split_axis=1, concat_axis=0, tiled=...  7.31 us
    all_to_all x1, waiting for transfers between devices, body(): lax.all_to_all(finished, 'expert', split_axis=0, concat_axis=0, tiled=True)  6.98 us
    ppermute x2, waiting for transfers between devices, body(): lax.ppermute(finding, axis_name='dp', perm=pages)  6.08 us
    all_to_all x1, waiting for transfers between devices, body(): lax.all_to_all(slot_inputs, 'expert', split_axis=1, concat_axis=0, tiled=...  5.75 us
    all_to_all x1, starting transfers between devices, body(): lax.all_to_all(finished, 'expert', split_axis=0, concat_axis=0, tiled=True)  5.53 us
    reduce_sum x2, other arithmetic, unit_rms(): jnp.mean(values * values, axis=axis_pos, keepdims=True) + norm_eps  3.35 us
    dot_general x1, matrix products, body(): jnp.einsum('rkf,kfd->rkd', hidden, down_weight, preferred_element_type=jn...  3.26 us
  transfers between devices with their start and end apart: 6, of which 5 were waited for; matrix products, arithmetic and copies ran while one was open for 4% of the time, Pallas kernels for 0%

profile of v1, /device:TPU:0, one launch (start us, length us, event | category | flops | bytes accessed | tf_op | source)
XLA Modules:
  0.0 90.2 jit_solution(12501815286602868935)
XLA Ops:
  6.5 0.0 copy-start
  7.3 1.0 %fusion.63 = f32[8]{0:T(128)S(1)} fusion(bf16[1280,8]{0,1:T(8,128)(2,1)} %param.8), kind=kLoop, calls=%fused_computation.63 | loop fusion | flops 30712 | bytes 20512 | tf_op jit(solution)/shard_map/reduce_sum | solution.py:17
  8.4 2.3 %fusion.2 = f32[4,256]{1,0:T(4,128)S(1)} fusion(bf16[4,256,1280]{2,1,0:T(8,128)(2,1)} %param.7), kind=kLoop, calls=%fused_computation.5 | loop fusion | flops 3931136 | bytes 2625536 | tf_op jit(solution)/shard_map/reduce_sum | solution.py:17
  10.7 0.0 copy-start.2
  10.7 2.6 %fusion.45 = f32[4,8,256]{2,1,0:T(8,128)S(1)} fusion(bf16[4,256,1280]{2,1,0:T(8,128)(2,1)} %param.7, f32[4,256]{1,0:T(4,128)S(1)} %add_rsqrt_fusion, bf16[1280,8]{0,1:T(8,128)(2,1)} %param.8, f32[8]{0:T(128)S(1)} %add_rsqrt_fusion.1, f32[]{:T(128)} %bitcast.106), kind=kOutput, calls=%fused_computation.33 | convolution fusion | flops 24950784 | bytes 2678820 | tf_op jit(solution)/shard_map/ipd,dn->inp/dot_general | solution.py:28
  13.3 0.2 fusion.72
  13.5 2.2 %convolution_convert_fusion.1 = bf16[4,8,1280]{2,1,0:T(8,128)(2,1)S(1)} fusion(bf16[4,256,1280]{2,1,0:T(8,128)(2,1)} %param.7, f32[4,8]{1,0:T(4,128)S(1)} %fusion.72, f32[4,8,256]{2,1,0:T(8,128)S(1)} %fusion.45), kind=kOutput, calls=%fused_computation.26 | convolution fusion | flops 21037344 | bytes 2736256 | tf_op jit(solution)/shard_map/inp,ipd->ind/dot_general | solution.py:34
  15.8 0.7 copy.12
  16.4 7.3 %all-to-all-start = ((bf16[4,8,1280]{2,0,1:T(4,128)(2,1)}), bf16[4,8,1280]{2,0,1:T(4,128)(2,1)S(1)}, u32[]{:S(2)}, u32[]{:S(2)}) async-start(bf16[4,8,1280]{2,0,1:T(4,128)(2,1)} %copy.12), calls=%async_computation | async-start | bytes 163840 | tf_op jit(solution)/shard_map/all_to_all | solution.py:37
  23.7 0.0 reduce-scatter.2.cloned.1.call-start
  23.8 0.6 pad_clamp_fusion
  24.4 0.0 copy-done.2
  24.4 0.6 convert_reduce_fusion.1
  25.0 5.8 %all-to-all-done = bf16[4,8,1280]{2,0,1:T(4,128)(2,1)S(1)} async-done(((bf16[4,8,1280]{2,0,1:T(4,128)(2,1)}), bf16[4,8,1280]{2,0,1:T(4,128)(2,1)S(1)}, u32[]{:S(2)}, u32[]{:S(2)}) %all-to-all-start) | async-done | bytes 81952 | tf_op jit(solution)/shard_map/all_to_all | solution.py:37
  30.8 0.1 collective-permute-start.2
  30.9 0.5 collective-permute-start
  31.4 0.0 copy-done
  31.4 0.7 fusion.29
  32.1 3.6 %collective-permute-done = bf16[32,1,1280]{2,0,1:T(8,128)(2,1)S(1)} collective-permute-done((bf16[32,1,1280]{2,0,1:T(8,128)(2,1)S(1)}, bf16[32,1,1280]{2,0,1:T(8,128)(2,1)S(1)}, u32[]{:S(2)}, u32[]{:S(2)}) %collective-permute-start) | collective-permute-done | bytes 81952 | tf_op jit(solution)/shard_map/ppermute | solution.py:47
  35.7 0.0 collective-permute-start.1
  35.7 0.7 fusion.26
  36.3 0.0 collective-permute-done.2
  36.3 0.7 fusion.32
  37.0 0.0 copy-start.1
  37.0 2.5 %collective-permute-done.1 = bf16[32,1,1280]{2,0,1:T(8,128)(2,1)S(1)} collective-permute-done((bf16[32,1,1280]{2,0,1:T(8,128)(2,1)S(1)}, bf16[32,1,1280]{2,0,1:T(8,128)(2,1)S(1)}, u32[]{:S(2)}, u32[]{:S(2)}) %collective-permute-start.1) | collective-permute-done | bytes 81952 | tf_op jit(solution)/shard_map/ppermute | solution.py:47
  39.5 0.7 fusion.23
  40.2 0.9 maximum_bitcast_fusion
  41.1 2.6 %gather_fusion = f32[4,32,1280]{2,1,0:T(8,128)} fusion(f32[4,32,1280]{2,1,0:T(8,128)} %maximum_bitcast_fusion, s32[1024]{0:T(1024)} %pad_clamp_fusion), kind=kCustom, calls=%fused_computation | custom fusion | bytes 1310736 | tf_op jit(solution)/shard_map/gather | solution.py:62
  43.7 0.0 copy-done.1
  43.7 2.5 %fusion.50 = bf16[4,32,1,1280]{3,1,0,2:T(8,128)(2,1)S(1)} fusion(f32[4,32,1280]{2,1,0:T(8,128)} %gather_fusion, f32[1280]{0:T(1024)S(1)} %copy-done.1), kind=kLoop, calls=%fused_computation.37 | loop fusion | flops 10813440 | bytes 988160 | tf_op jit(solution)/shard_map/convert_element_type | solution.py:65
  46.2 3.3 %fusion.20 = bf16[128,1,1280]{2,0,1:T(8,128)(2,1)} fusion(bf16[128,1280]{1,0:T(8,128)(2,1)S(1)} %bitcast.107, bf16[1,1280,1280]{2,1,0:T(8,128)(2,1)} %param.12), kind=kOutput, calls=%fused_computation.21 | convolution fusion | flops 419594240 | bytes 3932160 | tf_op jit(solution)/shard_map/rkf,kfd->rkd/dot_general | solution.py:67
  49.5 0.0 reduce-scatter.2.cloned.1.call-update
  49.5 0.8 convert_reduce_fusion
  50.3 16.5 %reduce-scatter.2.cloned.1.call-done = bf16[32,1,1280]{2,0,1:T(8,128)(2,1)} async-done(((bf16[128,1,1280]{2,0,1:T(8,128)(2,1)}), bf16[32,1,1280]{2,0,1:T(8,128)(2,1)}) %reduce-scatter.2.cloned.1.call-update) | async-done | bytes 81936 | tf_op jit(solution)/shard_map/reduce_scatter | solution.py:66
  66.8 0.9 %add_convert_fusion = bf16[32,1,1280]{2,0,1:T(8,128)(2,1)S(1)} fusion(bf16[32,1,1280]{2,0,1:T(8,128)(2,1)} %reduce-scatter.2.cloned.1.call-done, f32[1280]{0:T(1024)S(1)} %convert_reduce_fusion), kind=kLoop, calls=%fused_computation.55 | loop fusion | flops 122880 | bytes 168960 | tf_op jit(solution)/shard_map/convert_element_type | solution.py:78
  67.7 0.7 reshape.433
  68.4 5.5 %all-to-all-start.1 = ((bf16[8,4,1,1280]{3,1,2,0:T(4,128)(2,1)}), bf16[8,4,1,1280]{3,1,2,0:T(4,128)(2,1)S(1)}, u32[]{:S(2)}, u32[]{:S(2)}) async-start(bf16[8,4,1,1280]{3,1,2,0:T(4,128)(2,1)} %bitcast.34), calls=%async_computation.2 | async-start | bytes 163840 | tf_op jit(solution)/shard_map/all_to_all | solution.py:80
  73.9 7.0 %all-to-all-done.1 = bf16[8,4,1,1280]{3,1,2,0:T(4,128)(2,1)S(1)} async-done(((bf16[8,4,1,1280]{3,1,2,0:T(4,128)(2,1)}), bf16[8,4,1,1280]{3,1,2,0:T(4,128)(2,1)S(1)}, u32[]{:S(2)}, u32[]{:S(2)}) %all-to-all-start.1) | async-done | bytes 81952 | tf_op jit(solution)/shard_map/all_to_all | solution.py:80
  80.9 2.4 %convolution_convert_fusion = bf16[4,256,1280]{2,1,0:T(8,128)(2,1)} fusion(bf16[8,4,1,1280]{3,1,2,0:T(4,128)(2,1)S(1)} %all-to-all-done.1, f32[4,256]{1,0:T(4,128)S(1)} %fusion.73, f32[4,8,256]{2,1,0:T(8,128)S(1)} %fusion.45), kind=kOutput, calls=%fused_computation.7 | convolution fusion | flops 22307848 | bytes 2740224 | tf_op jit(solution)/shard_map/iekp,eikd->ipd/dot_general | solution.py:82
  (6 shorter events, 0.1 us)
Async XLA Ops:
  6.5 24.8 %copy-start = (bf16[1,1280,1280]{2,1,0:T(8,128)(2,1)S(1)}, bf16[1,1280,1280]{2,1,0:T(8,128)(2,1)}, u32[]{:S(2)}) copy-start(bf16[1,1280,1280]{2,1,0:T(8,128)(2,1)} %param.10) | copy-start | bytes 9830404
  10.7 13.7 %copy-start.2 = (bf16[1,1280]{1,0:T(2,128)(2,1)S(1)}, bf16[1,1280]{1,0:T(2,128)(2,1)}, u32[]{:S(2)}) copy-start(bf16[1,1280]{1,0:T(2,128)(2,1)} %param.11) | copy-start | bytes 7684
  16.4 14.3 %all-to-all-start = ((bf16[4,8,1280]{2,0,1:T(4,128)(2,1)}), bf16[4,8,1280]{2,0,1:T(4,128)(2,1)S(1)}, u32[]{:S(2)}, u32[]{:S(2)}) async-start(bf16[4,8,1280]{2,0,1:T(4,128)(2,1)} %copy.12), calls=%async_computation | async-start | bytes 163840 | tf_op jit(solution)/shard_map/all_to_all | solution.py:37
  23.7 43.1 %reduce-scatter.2.cloned.1.call-start = ((), (), s32[]{:S(2)}) async-start(), calls=%async_computation.3 | async-start | bytes 409600 | tf_op jit(solution)/shard_map/reduce_scatter | solution.py:66
  30.8 5.5 %collective-permute-start.2 = (bf16[32,1,1280]{2,0,1:T(8,128)(2,1)S(1)}, bf16[32,1,1280]{2,0,1:T(8,128)(2,1)S(1)}, u32[]{:S(2)}, u32[]{:S(2)}) collective-permute-start(bf16[32,1,1280]{2,0,1:T(8,128)(2,1)S(1)} %all_to_all.19), channel_id=1, source_target_pairs={{0,24},{8,0},{16,8},{24,16},{1,25},{9,1},{17,9},{25,17},{2,26},{10... | collective-permute-start | bytes 245768 | tf_op jit(solution)/shard_map/ppermute | solution.py:49
  30.9 4.8 %collective-permute-start = (bf16[32,1,1280]{2,0,1:T(8,128)(2,1)S(1)}, bf16[32,1,1280]{2,0,1:T(8,128)(2,1)S(1)}, u32[]{:S(2)}, u32[]{:S(2)}) collective-permute-start(bf16[32,1,1280]{2,0,1:T(8,128)(2,1)S(1)} %all_to_all.19), channel_id=1, source_target_pairs={{0,8},{8,16},{16,24},{24,0},{1,9},{9,17},{17,25},{25,1},{2,10},{10... | collective-permute-start | bytes 245768 | tf_op jit(solution)/shard_map/ppermute | solution.py:47
  35.7 3.9 %collective-permute-start.1 = (bf16[32,1,1280]{2,0,1:T(8,128)(2,1)S(1)}, bf16[32,1,1280]{2,0,1:T(8,128)(2,1)S(1)}, u32[]{:S(2)}, u32[]{:S(2)}) collective-permute-start(bf16[32,1,1280]{2,0,1:T(8,128)(2,1)S(1)} %collective-permute-done), channel_id=1, source_target_pairs={{0,8},{8,16},{16,24},{24,0},{1,9},{9,17},{17,25},{25,1},{2,10},{10... | collective-permute-start | bytes 245768 | tf_op jit(solution)/shard_map/ppermute | solution.py:47
  37.0 6.7 %copy-start.1 = (f32[1280]{0:T(1024)S(1)}, f32[1280]{0:T(1024)}, u32[]{:S(2)}) copy-start(f32[1280]{0:T(1024)} %convert_reduce_fusion.1) | copy-start | bytes 15364
  68.4 12.5 %all-to-all-start.1 = ((bf16[8,4,1,1280]{3,1,2,0:T(4,128)(2,1)}), bf16[8,4,1,1280]{3,1,2,0:T(4,128)(2,1)S(1)}, u32[]{:S(2)}, u32[]{:S(2)}) async-start(bf16[8,4,1,1280]{3,1,2,0:T(4,128)(2,1)} %bitcast.34), calls=%async_computation.2 | async-start | bytes 163840 | tf_op jit(solution)/shard_map/all_to_all | solution.py:80
Sparse Core Ops, SparseCore 0:
  49.6 17.1 reduce-scatter.1
